TPU v7x, 32 devices: a whole 2x2x4 slice. The times are simulated.
32 devices in a mesh: section: 2 (over y), freq: 16 (over z, x, core).
Axes of the slice: x: 2, y: 2, z: 4, core: 2. Of those that a mesh axis runs over, the one named last changes fastest.
Arguments:
- spectra: float32 [4, 16, 131072], P('section', None, 'freq'), may hold values from 0.1 to 90, as said below
- channel_gain: float32 [131072], P('freq'), may hold values from 0.5 to 2
- bandpass_bin: int32 [131072], P('freq'), may hold values from 0 to 63, never falling along the last dimension, each value on 1 to 8192 neighbouring positions
- drift_range: int32 [4], replicated, may hold values from 1 to 2, as said below
- hit_cutoff: int32 [4, 2, 16], replicated, may hold values from 0 to 1023
Outputs:
- drift_score: float32 [4, 2, 131072], P(None, 'section', 'freq')
Inputs may be any that keep to these rules, and one draw needn't show every extreme that they name: `spectra`: every entry is positive. `bandpass_bin`: the bins never fall along the channels and each of the 64 bins holds 1 to 8192 channels. `drift_range`: some group reaches 2 and some other group searches stride 1 only.
All inputs are finite; a program needn't handle non-finite values.
Results may differ from a plain program's by a relative error of at most 0.0003.
Values sent between devices are 32-bit elements; how exact they have to be, the bound alone decides.
No kernel may reach another device: no remote copies, remote signals or barrier semaphores. Data moves between devices by JAX's collectives and lax.ppermute only.
A program may use at most 64 MiB of HBM per device.

v0:
```python
import jax
import jax.numpy as jnp
from jax import lax
from jax.sharding import PartitionSpec as P


def carried_in(value, axis, join, neutral):
    count, mine = (lax.axis_size(axis), lax.axis_index(axis))
    pieces = jax.tree.map(lambda part: lax.all_gather(part, axis), value)
    subtotal = jax.tree.map(
        lambda part, zero: jnp.full_like(part, 0) + jnp.asarray(zero, part.dtype), value, neutral
    )

    def turn(position, subtotal):
        longer = join(subtotal, jax.tree.map(lambda part: part[position], pieces))
        return jax.tree.map(lambda new, old: jnp.where(position < mine, new, old), longer, subtotal)

    return lax.fori_loop(0, count - 1, turn, subtotal)


def passed_along(block, axis, distance):
    devices = range(lax.axis_size(axis))
    route = [(i - distance, i) for i in devices if i - distance in devices]
    return lax.ppermute(block, axis, route)


def taylor_tree(extended, stride, margin):
    length = extended.shape[-1]
    current = extended[:, None, :]
    blocks_width = 1
    while current.shape[0] > 1:
        former = current[0::2]
        latter = jnp.pad(current[1::2], ((0, 0), (0, 0), (0, margin)))
        merged = []
        for half_idx in range(blocks_width):
            anchor = former[:, half_idx]
            source = latter[:, half_idx]
            merged.append(
                anchor + lax.dynamic_slice_in_dim(source, half_idx * stride, length, axis=1)
            )
            merged.append(
                anchor + lax.dynamic_slice_in_dim(source, (half_idx + 1) * stride, length, axis=1)
            )
        current = jnp.stack(merged, axis=1)
        blocks_width = blocks_width * 2
    return current[0]


def score_rate(extended, stride, cut_row, chan_dev, margin):
    drifts = taylor_tree(extended, stride, margin)[:, :chan_dev]
    cut_levels = cut_row.astype(jnp.float32) / 256.0
    return jnp.mean(jax.nn.relu(0.25 * drifts - cut_levels[:, None]), axis=0)


def block_layout(chan_dev):
    width = min(1024, chan_dev)
    return (width, chan_dev // width)


def bin_partials(summed, bandpass_bin, total_bins, integrations):
    group_dev, chan_dev = summed.shape
    width, blocks = block_layout(chan_dev)
    bins_iota = jnp.arange(total_bins, dtype=jnp.int32)
    values = jnp.transpose(summed.reshape(group_dev, blocks, width), (1, 0, 2))
    indices = bandpass_bin.reshape(blocks, width)

    def bin_one_block(carry, items):
        block_values, block_index = items
        one_hot = (block_index[:, None] == bins_iota[None, :]).astype(jnp.float32)
        sums = carry[0] + jnp.dot(
            block_values,
            one_hot,
            precision=lax.Precision.HIGHEST,
            preferred_element_type=jnp.float32,
        )
        counts = carry[1] + jnp.sum(one_hot, axis=0)
        return ((sums, counts), None)

    start = (jnp.zeros((group_dev, total_bins), jnp.float32), jnp.zeros((total_bins,), jnp.float32))
    (bin_sums, counts), unused = lax.scan(bin_one_block, start, (values, indices))
    tallies = jnp.broadcast_to(float(integrations) * counts[None, :], bin_sums.shape)
    return (bin_sums, tallies)


def read_levels(running, bandpass_bin):
    group_dev, total_bins = running.shape
    chan_dev = bandpass_bin.shape[0]
    width, blocks = block_layout(chan_dev)
    bins_iota = jnp.arange(total_bins, dtype=jnp.int32)

    def read_one_block(carry, block_index):
        one_hot = (block_index[:, None] == bins_iota[None, :]).astype(jnp.float32)
        picked = lax.dot_general(
            running,
            one_hot,
            (((1,), (1,)), ((), ())),
            precision=lax.Precision.HIGHEST,
            preferred_element_type=jnp.float32,
        )
        return (carry, picked)

    unused, picked_blocks = lax.scan(read_one_block, 0, bandpass_bin.reshape(blocks, width))
    return jnp.transpose(picked_blocks, (1, 0, 2)).reshape(group_dev, chan_dev)


def add_pair(earlier, later):
    return (earlier[0] + later[0], earlier[1] + later[1])


def shards(spectra, channel_gain, bandpass_bin, drift_range, hit_cutoff):
    group_dev, integrations, chan_dev = spectra.shape
    total_bins = 4 * lax.axis_size("freq")
    calibrated = spectra * channel_gain[None, None, :]
    summed = jnp.sum(calibrated, axis=1)
    bin_sums, tallies = bin_partials(summed, bandpass_bin, total_bins, integrations)
    freq_sums, freq_tallies = lax.psum((bin_sums, tallies), "freq")
    zero_row = jnp.zeros((total_bins,), jnp.float32)
    before_sums, before_tallies = carried_in(
        (jnp.sum(freq_sums, axis=0), jnp.sum(freq_tallies, axis=0)),
        "section",
        add_pair,
        (zero_row, zero_row),
    )
    running = (before_sums[None, :] + jnp.cumsum(freq_sums, axis=0)) / (
        before_tallies[None, :] + jnp.cumsum(freq_tallies, axis=0)
    )
    levels = read_levels(running, bandpass_bin)
    normal = calibrated / levels[:, None, :] - 1.0
    rate_count = hit_cutoff.shape[1]
    margin = rate_count * (integrations - 1)
    right_rim = passed_along(normal[:, :, :margin], "freq", -1)
    section_first = lax.axis_index("section") * group_dev

    def one_group(position, scores):
        extended = jnp.concatenate([normal[position], right_rim[position]], axis=1)
        group_id = section_first + position
        for stride in range(1, rate_count + 1):
            result_row = lax.cond(
                stride <= drift_range[group_id],
                lambda: score_rate(
                    extended, stride, hit_cutoff[group_id, stride - 1], chan_dev, margin
                ),
                lambda: jnp.zeros((chan_dev,), jnp.float32),
            )
            scores = scores.at[position, stride - 1].set(result_row)
        return scores

    own_scores = lax.fori_loop(
        0, group_dev, one_group, jnp.zeros((group_dev, rate_count, chan_dev), jnp.float32)
    )
    return lax.all_to_all(own_scores, "section", split_axis=1, concat_axis=0, tiled=True)


def solution(mesh):
    return jax.shard_map(
        shards,
        mesh=mesh,
        in_specs=(P("section", None, "freq"), P("freq"), P("freq"), P(), P()),
        out_specs=P(None, "section", "freq"),
        check_vma=False,
    )
```

profile of v0, /device:TPU:0, one launch (start us, length us, event | category | flops | bytes accessed | tf_op | source)
XLA Modules:
  0.0 124.3 jit_solution(13200664469159023011)
XLA Ops:
  0.8 1.6 %multiply_reduce_fusion = f32[2,8192]{1,0:T(2,128)S(1)} fusion(f32[2,16,8192]{2,1,0:T(8,128)} %param.19, f32[8192]{0:T(1024)S(1)} %copy-done.1), kind=kLoop, calls=%fused_computation.218 | loop fusion | flops 507904 | bytes 1146880 | tf_op jit(solution)/shard_map/reduce_sum | solution.py:114
  2.4 3.4 %while.47 = (s32[]{:T(128)}, f32[2,64]{1,0:T(2,128)S(1)}, f32[64]{0:T(128)S(1)}, f32[8,2,1024]{2,1,0:T(2,128)S(1)}, s32[8,1024]{1,0:T(8,128)S(1)}, /*index=5*/s32[]{:T(128)}, s32[]{:T(128)}) while((s32[]{:T(128)}, f32[2,64]{1,0:T(2,128)S(1)}, f32[64]{0:T(128)S(1)}, f32[8,2,1024]{2,1,0:T(2,128)S(1)}, s32[8,1024]{1,0:T(8,128)S(1)}, ...), condition=%wide.region_3.4_spmd.clone, body=%wide.region_1.3_spmd.clone.sunk | while | flops 1835331 | bytes 27232 | solution.py:80
  5.8 34.9 %all-reduce.10 = (f32[2,64]{1,0:T(2,128)S(1)}, f32[2,64]{1,0:T(2,128)S(1)}) all-reduce(f32[2,64]{1,0:T(2,128)S(1)} %broadcast_in_dim.43, f32[2,64]{1,0:T(2,128)S(1)} %get-tuple-element.288), channel_id=1, replica_groups=mesh['section'=2,'freq'=16] {'freq'}, use_global_device_ids=true, to_apply=%region_7.8 | all-reduce | flops 256 | bytes 2048 | tf_op jit(solution)/shard_map/psum | solution.py:116
  43.1 4.9 %all-reduce.11 = (f32[128]{0:T(128)S(1)}, f32[128]{0:T(128)S(1)}) all-reduce(f32[128]{0:T(128)S(1)} %dynamic-update-slice.15, f32[128]{0:T(128)S(1)} %dynamic-update-slice.14), channel_id=3, replica_groups=mesh['section'=2,'freq'=16] {'section'}, use_global_device_ids=true, to_apply=%add.9 | all-reduce | flops 256 | bytes 2048
  48.1 3.8 %while.46 = (s32[]{:T(128)}, f32[8,2,1024]{2,1,0:T(2,128)S(1)}, s32[8,1024]{1,0:T(8,128)S(1)}, f32[2,64]{1,0:T(2,128)S(1)}, s32[]{:T(128)}) while((s32[]{:T(128)}, f32[8,2,1024]{2,1,0:T(2,128)S(1)}, s32[8,1024]{1,0:T(8,128)S(1)}, f32[2,64]{1,0:T(2,128)S(1)}, s32[]{:T(128)}) %tuple.198), condition=%wide.region_11.12_spmd.clone, body=%wide.region_10.11_spmd.clone.sunk | while | flops 1638402 | bytes 21573 | solution.py:102
  52.1 1.3 %collective-permute-start = (f32[2,16,30]{2,1,0:T(8,128)S(1)}, f32[2,16,30]{2,1,0:T(8,128)S(1)}, u32[]{:S(2)}, u32[]{:S(2)}) collective-permute-start(f32[2,16,30]{2,1,0:T(8,128)S(1)} %slice.378), channel_id=1, source_target_pairs={{1,0},{2,1},{3,2},{4,3},{5,4},{6,5},{7,6},{8,7},{9,8},{10,9},{11,1... | collective-permute-start | bytes 11528 | tf_op jit(solution)/shard_map/ppermute | solution.py:24
  53.4 1.8 %collective-permute-done = f32[2,16,30]{2,1,0:T(8,128)S(1)} collective-permute-done((f32[2,16,30]{2,1,0:T(8,128)S(1)}, f32[2,16,30]{2,1,0:T(8,128)S(1)}, u32[]{:S(2)}, u32[]{:S(2)}) %collective-permute-start) | collective-permute-done | bytes 3872 | tf_op jit(solution)/shard_map/ppermute | solution.py:24
  55.2 61.3 %while.45 = (s32[]{:T(128)}, f32[2,2,8192]{2,1,0:T(2,128)S(1)}, s32[]{:T(128)}, s32[4]{0:T(128)S(1)}, f32[2,16,8192]{2,1,0:T(8,128)S(1)}, /*index=5*/f32[2,16,30...) while((s32[]{:T(128)}, f32[2,2,8192]{2,1,0:T(2,128)S(1)}, ...), condition=%wide.region_21.22_spmd, body=%wide.region_12.21_spmd.sunk | while | flops 3301456 | bytes 33727040 | solution.py:148
  56.6 17.2 %conditional.4 = (f32[1,1,8192]{2,1,0:T(1,128)S(1)}) conditional(s32[]{:T(128)} %bitcast.327, () %tuple.180, (f32[16,8222]{1,0:T(8,128)S(1)}, s32[]{:T(128)}, s32[4,2,16]{2,1,0:T(2,128)}) %tuple.181), branch_computations={%region_14.14_spmd, %region_15.16_spmd} | conditional | flops 1576738 | bytes 15647118 | solution.py:138
  56.6 0.9 slice.271
  57.6 0.9 slice.270
  58.8 1.7 %slice.274 = f32[4,2,8222]{2,0,1:T(4,128)S(1)} slice(f32[8,2,8222]{2,0,1:T(8,128)S(1)} %pad_maximum_fusion), slice={[1:8:2], [0:2:1], [0:8222:1]} | slice | bytes 526208 | tf_op jit(solution)/shard_map/while/body/eval_jaxpr/cond/branch_1_fun/slice | solution.py:33
  60.5 1.7 %slice.272 = f32[4,2,8222]{2,0,1:T(4,128)S(1)} slice(f32[8,2,8222]{2,0,1:T(8,128)S(1)} %pad_maximum_fusion), slice={[0:8:2], [0:2:1], [0:8222:1]} | slice | bytes 526208 | tf_op jit(solution)/shard_map/while/body/eval_jaxpr/cond/branch_1_fun/slice | solution.py:32
  62.5 2.2 %slice.280 = f32[2,4,8222]{2,0,1:T(2,128)S(1)} slice(f32[4,4,8222]{2,0,1:T(4,128)S(1)} %pad_maximum_fusion.1), slice={[1:4:2], [0:4:1], [0:8222:1]} | slice | bytes 526208 | tf_op jit(solution)/shard_map/while/body/eval_jaxpr/cond/branch_1_fun/slice | solution.py:33
  64.8 2.2 %slice.278 = f32[2,4,8222]{2,0,1:T(2,128)S(1)} slice(f32[4,4,8222]{2,0,1:T(4,128)S(1)} %pad_maximum_fusion.1), slice={[0:4:2], [0:4:1], [0:8222:1]} | slice | bytes 526208 | tf_op jit(solution)/shard_map/while/body/eval_jaxpr/cond/branch_1_fun/slice | solution.py:32
  69.8 3.0 %stack.169 = f32[1,16,8222]{2,1,0:T(8,128)S(1)} concatenate(f32[1,1,8222]{2,1,0:T(1,128)S(1)} %get-tuple-element.436, f32[1,1,8222]{2,1,0:T(1,128)S(1)} %get-tuple-element.437, f32[1,1,8222]{2,1,0:T(1,128)S(1)} %get-tuple-element.427, f32[1,1,8222]{2,1,0:T(1,128)S(1)} %get-tuple-element.426, f32[1,1,8222]{2,1,0:T(1,128)S(1)} %get-tuple-element.434, ...), dimensions={1} | concatenate | bytes 1052416 | tf_op jit(solution)/shard_map/while/body/eval_jaxpr/cond/branch_1_fun/stack | solution.py:44
  78.7 17.2 %conditional.4 = (f32[1,1,8192]{2,1,0:T(1,128)S(1)}) conditional(s32[]{:T(128)} %bitcast.327, () %tuple.180, (f32[16,8222]{1,0:T(8,128)S(1)}, s32[]{:T(128)}, s32[4,2,16]{2,1,0:T(2,128)}) %tuple.181), branch_computations={%region_14.14_spmd, %region_15.16_spmd} | conditional | flops 1576738 | bytes 15647118 | solution.py:138
  78.7 0.9 slice.271
  79.7 0.9 slice.270
  80.8 1.7 %slice.274 = f32[4,2,8222]{2,0,1:T(4,128)S(1)} slice(f32[8,2,8222]{2,0,1:T(8,128)S(1)} %pad_maximum_fusion), slice={[1:8:2], [0:2:1], [0:8222:1]} | slice | bytes 526208 | tf_op jit(solution)/shard_map/while/body/eval_jaxpr/cond/branch_1_fun/slice | solution.py:33
  82.5 1.7 %slice.272 = f32[4,2,8222]{2,0,1:T(4,128)S(1)} slice(f32[8,2,8222]{2,0,1:T(8,128)S(1)} %pad_maximum_fusion), slice={[0:8:2], [0:2:1], [0:8222:1]} | slice | bytes 526208 | tf_op jit(solution)/shard_map/while/body/eval_jaxpr/cond/branch_1_fun/slice | solution.py:32
  84.6 2.2 %slice.280 = f32[2,4,8222]{2,0,1:T(2,128)S(1)} slice(f32[4,4,8222]{2,0,1:T(4,128)S(1)} %pad_maximum_fusion.1), slice={[1:4:2], [0:4:1], [0:8222:1]} | slice | bytes 526208 | tf_op jit(solution)/shard_map/while/body/eval_jaxpr/cond/branch_1_fun/slice | solution.py:33
  86.8 2.2 %slice.278 = f32[2,4,8222]{2,0,1:T(2,128)S(1)} slice(f32[4,4,8222]{2,0,1:T(4,128)S(1)} %pad_maximum_fusion.1), slice={[0:4:2], [0:4:1], [0:8222:1]} | slice | bytes 526208 | tf_op jit(solution)/shard_map/while/body/eval_jaxpr/cond/branch_1_fun/slice | solution.py:32
  91.9 3.0 %stack.169 = f32[1,16,8222]{2,1,0:T(8,128)S(1)} concatenate(f32[1,1,8222]{2,1,0:T(1,128)S(1)} %get-tuple-element.436, f32[1,1,8222]{2,1,0:T(1,128)S(1)} %get-tuple-element.437, f32[1,1,8222]{2,1,0:T(1,128)S(1)} %get-tuple-element.427, f32[1,1,8222]{2,1,0:T(1,128)S(1)} %get-tuple-element.426, f32[1,1,8222]{2,1,0:T(1,128)S(1)} %get-tuple-element.434, ...), dimensions={1} | concatenate | bytes 1052416 | tf_op jit(solution)/shard_map/while/body/eval_jaxpr/cond/branch_1_fun/stack | solution.py:44
  98.3 17.2 %conditional.5 = (f32[1,1,8192]{2,1,0:T(1,128)S(1)}) conditional(s32[]{:T(128)} %bitcast.329, () %tuple.182, (f32[16,8222]{1,0:T(8,128)S(1)}, s32[]{:T(128)}, s32[4,2,16]{2,1,0:T(2,128)}) %tuple.181), branch_computations={%region_18.18_spmd, %region_19.20_spmd} | conditional | flops 1576738 | bytes 15647118 | solution.py:138
  98.4 0.9 slice.307
  100.5 1.7 %slice.310 = f32[4,2,8222]{2,0,1:T(4,128)S(1)} slice(f32[8,2,8222]{2,0,1:T(8,128)S(1)} %pad_maximum_fusion.2), slice={[1:8:2], [0:2:1], [0:8222:1]} | slice | bytes 526208 | tf_op jit(solution)/shard_map/while/body/eval_jaxpr/cond/branch_1_fun/slice | solution.py:33
  102.2 1.7 %slice.308 = f32[4,2,8222]{2,0,1:T(4,128)S(1)} slice(f32[8,2,8222]{2,0,1:T(8,128)S(1)} %pad_maximum_fusion.2), slice={[0:8:2], [0:2:1], [0:8222:1]} | slice | bytes 526208 | tf_op jit(solution)/shard_map/while/body/eval_jaxpr/cond/branch_1_fun/slice | solution.py:32
  104.3 2.2 %slice.316 = f32[2,4,8222]{2,0,1:T(2,128)S(1)} slice(f32[4,4,8222]{2,0,1:T(4,128)S(1)} %pad_maximum_fusion.3), slice={[1:4:2], [0:4:1], [0:8222:1]} | slice | bytes 526208 | tf_op jit(solution)/shard_map/while/body/eval_jaxpr/cond/branch_1_fun/slice | solution.py:33
  106.5 2.2 %slice.314 = f32[2,4,8222]{2,0,1:T(2,128)S(1)} slice(f32[4,4,8222]{2,0,1:T(4,128)S(1)} %pad_maximum_fusion.3), slice={[0:4:2], [0:4:1], [0:8222:1]} | slice | bytes 526208 | tf_op jit(solution)/shard_map/while/body/eval_jaxpr/cond/branch_1_fun/slice | solution.py:32
  111.6 3.0 %stack.203 = f32[1,16,8222]{2,1,0:T(8,128)S(1)} concatenate(f32[1,1,8222]{2,1,0:T(1,128)S(1)} %get-tuple-element.482, f32[1,1,8222]{2,1,0:T(1,128)S(1)} %get-tuple-element.483, f32[1,1,8222]{2,1,0:T(1,128)S(1)} %get-tuple-element.473, f32[1,1,8222]{2,1,0:T(1,128)S(1)} %get-tuple-element.472, f32[1,1,8222]{2,1,0:T(1,128)S(1)} %get-tuple-element.480, ...), dimensions={1} | concatenate | bytes 1052416 | tf_op jit(solution)/shard_map/while/body/eval_jaxpr/cond/branch_1_fun/stack | solution.py:44
  116.6 6.8 %all_to_all.19 = f32[2,2,8192]{2,0,1:T(2,128)S(1)} all-to-all(f32[2,2,8192]{2,0,1:T(2,128)S(1)} %copy.9), channel_id=1, replica_groups=mesh['section'=2,'freq'=16] {'section'}, dimensions={1} | all-to-all | bytes 262144 | tf_op jit(solution)/shard_map/all_to_all | solution.py:151
  (173 shorter events, 31.6 us)
Async XLA Ops:
  0.0 0.8 copy-start.1
  0.8 51.1 %copy-start = (f32[2,16,8192]{2,1,0:T(8,128)S(1)}, f32[2,16,8192]{2,1,0:T(8,128)}, u32[]{:S(2)}) copy-start(f32[2,16,8192]{2,1,0:T(8,128)} %param.19) | copy-start | bytes 3145732
  40.8 0.7 copy-start.4
  52.1 3.1 %collective-permute-start = (f32[2,16,30]{2,1,0:T(8,128)S(1)}, f32[2,16,30]{2,1,0:T(8,128)S(1)}, u32[]{:S(2)}, u32[]{:S(2)}) collective-permute-start(f32[2,16,30]{2,1,0:T(8,128)S(1)} %slice.378), channel_id=1, source_target_pairs={{1,0},{2,1},{3,2},{4,3},{5,4},{6,5},{7,6},{8,7},{9,8},{10,9},{11,1... | collective-permute-start | bytes 11528 | tf_op jit(solution)/shard_map/ppermute | solution.py:24
  53.4 1.8 %copy-start.2 = (s32[3]{0:T(128)S(1)}, s32[3]{0:T(128)}, u32[]{:S(2)}) copy-start(s32[3]{0:T(128)} %constant.199.clone.1) | copy-start | bytes 40
  53.4 1.8 %copy-start.3 = (s32[4]{0:T(128)S(1)}, s32[4]{0:T(128)}, u32[]{:S(2)}) copy-start(s32[4]{0:T(128)} %param.22) | copy-start | bytes 52
where the time goes:
time: 125 us; the launch traced here: 124 us
  blocking collectives  46.7 us (37%)
  local copies, waits for them, and re-layouts  45.2 us (36%)
  other arithmetic  19.7 us (16%)
  matrix products  5.12 us (4%)
  loops' own time  3.79 us (3%)
  waiting for transfers between devices  1.75 us (1%)
  starting transfers between devices  1.29 us (1%)
    psum x1, blocking collectives, shards(): freq_sums, freq_tallies = lax.psum((bin_sums, tallies), 'freq')  34.9 us
    slice x12, local copies, waits for them, and re-layouts, taylor_tree(): latter = jnp.pad(current[1::2], ((0, 0), (0, 0), (0, margin)))  15.2 us
    slice x9, local copies, waits for them, and re-layouts, taylor_tree(): former = current[0::2]  14.4 us
    another operation x3, local copies, waits for them, and re-layouts, taylor_tree(): current = jnp.stack(merged, axis=1)  9.09 us
    all_to_all x1, blocking collectives, shards(): lax.all_to_all(own_scores, 'section', split_axis=1, concat_axis=0, tiled=...  6.85 us
    another operation x27, other arithmetic, taylor_tree(): current = jnp.stack(merged, axis=1)  6.26 us
    unnamed x1, blocking collectives  4.91 us
    another operation x6, other arithmetic  4.22 us
  transfers between devices with their start and end apart: 1, of which 1 were waited for; matrix products, arithmetic and copies ran while one was open for 0% of the time, Pallas kernels for 0%

commit v1 on v0

--- a/solution.py
+++ b/solution.py
@@ -2,6 +2,13 @@
 import jax.numpy as jnp
 from jax import lax
 from jax.sharding import PartitionSpec as P
+
+
+def exchange_blocks(shard, name, split, join):
+    size = lax.axis_size(name)
+    blocks = jnp.stack(jnp.split(shard, size, axis=split), axis=0)
+    blocks = lax.all_to_all(blocks, name, split_axis=0, concat_axis=0)
+    return jnp.concatenate(blocks, axis=join)
 
 
 def carried_in(value, axis, join, neutral):
@@ -148,7 +155,7 @@
     own_scores = lax.fori_loop(
         0, group_dev, one_group, jnp.zeros((group_dev, rate_count, chan_dev), jnp.float32)
     )
-    return lax.all_to_all(own_scores, "section", split_axis=1, concat_axis=0, tiled=True)
+    return exchange_blocks(own_scores, "section", 1, 0)
 
 
 def solution(mesh):

time: 125 us -> 125 us (level)
    another operation x6 -> x7, other arithmetic: 4.22 us -> 4.63 us
where the time goes in v1:
time: 125 us; the launch traced here: 124 us
  blocking collectives  46.7 us (37%)
  local copies, waits for them, and re-layouts  44.9 us (36%)
  other arithmetic  20.1 us (16%)
  matrix products  5.12 us (4%)
  loops' own time  3.43 us (3%)
  waiting for transfers between devices  1.75 us (1%)
  starting transfers between devices  1.29 us (1%)
    psum x1, blocking collectives, shards(): freq_sums, freq_tallies = lax.psum((bin_sums, tallies), 'freq')  34.9 us
    slice x12, local copies, waits for them, and re-layouts, taylor_tree(): latter = jnp.pad(current[1::2], ((0, 0), (0, 0), (0, margin)))  15.2 us
    slice x9, local copies, waits for them, and re-layouts, taylor_tree(): former = current[0::2]  14.4 us
    another operation x3, local copies, waits for them, and re-layouts, taylor_tree(): current = jnp.stack(merged, axis=1)  9.09 us
    all_to_all x1, blocking collectives, exchange_blocks(): blocks = lax.all_to_all(blocks, name, split_axis=0, concat_axis=0)  6.85 us
    another operation x27, other arithmetic, taylor_tree(): current = jnp.stack(merged, axis=1)  6.26 us
    unnamed x1, blocking collectives  4.91 us
    another operation x6, other arithmetic  4.51 us
  transfers between devices with their start and end apart: 1, of which 1 were waited for; matrix products, arithmetic and copies ran while one was open for 0% of the time, Pallas kernels for 0%

profile of v1, /device:TPU:0, one launch (start us, length us, event | category | flops | bytes accessed | tf_op | source)
XLA Modules:
  0.0 124.1 jit_solution(5124658437611934114)
XLA Ops:
  0.8 1.6 %multiply_reduce_fusion = f32[2,8192]{1,0:T(2,128)S(1)} fusion(f32[2,16,8192]{2,1,0:T(8,128)} %param.19, f32[8192]{0:T(1024)S(1)} %copy-done.1), kind=kLoop, calls=%fused_computation.218 | loop fusion | flops 507904 | bytes 1146880 | tf_op jit(solution)/shard_map/reduce_sum | solution.py:121
  2.4 3.4 %while.47 = (s32[]{:T(128)}, f32[2,64]{1,0:T(2,128)S(1)}, f32[64]{0:T(128)S(1)}, f32[8,2,1024]{2,1,0:T(2,128)S(1)}, s32[8,1024]{1,0:T(8,128)S(1)}, /*index=5*/s32[]{:T(128)}, s32[]{:T(128)}) while((s32[]{:T(128)}, f32[2,64]{1,0:T(2,128)S(1)}, f32[64]{0:T(128)S(1)}, f32[8,2,1024]{2,1,0:T(2,128)S(1)}, s32[8,1024]{1,0:T(8,128)S(1)}, ...), condition=%wide.region_3.4_spmd.clone, body=%wide.region_1.3_spmd.clone.sunk | while | flops 1835331 | bytes 27232 | solution.py:87
  5.8 34.9 %all-reduce.10 = (f32[2,64]{1,0:T(2,128)S(1)}, f32[2,64]{1,0:T(2,128)S(1)}) all-reduce(f32[2,64]{1,0:T(2,128)S(1)} %broadcast_in_dim.43, f32[2,64]{1,0:T(2,128)S(1)} %get-tuple-element.288), channel_id=1, replica_groups=mesh['section'=2,'freq'=16] {'freq'}, use_global_device_ids=true, to_apply=%region_7.8 | all-reduce | flops 256 | bytes 2048 | tf_op jit(solution)/shard_map/psum | solution.py:123
  43.2 4.9 %all-reduce.11 = (f32[128]{0:T(128)S(1)}, f32[128]{0:T(128)S(1)}) all-reduce(f32[128]{0:T(128)S(1)} %dynamic-update-slice.15, f32[128]{0:T(128)S(1)} %dynamic-update-slice.14), channel_id=3, replica_groups=mesh['section'=2,'freq'=16] {'section'}, use_global_device_ids=true, to_apply=%add.9 | all-reduce | flops 256 | bytes 2048
  48.1 3.8 %while.46 = (s32[]{:T(128)}, f32[8,2,1024]{2,1,0:T(2,128)S(1)}, s32[8,1024]{1,0:T(8,128)S(1)}, f32[2,64]{1,0:T(2,128)S(1)}, s32[]{:T(128)}) while((s32[]{:T(128)}, f32[8,2,1024]{2,1,0:T(2,128)S(1)}, s32[8,1024]{1,0:T(8,128)S(1)}, f32[2,64]{1,0:T(2,128)S(1)}, s32[]{:T(128)}) %tuple.199), condition=%wide.region_11.12_spmd.clone, body=%wide.region_10.11_spmd.clone.sunk | while | flops 1638402 | bytes 21573 | solution.py:109
  52.1 1.3 %collective-permute-start = (f32[2,16,30]{2,1,0:T(8,128)S(1)}, f32[2,16,30]{2,1,0:T(8,128)S(1)}, u32[]{:S(2)}, u32[]{:S(2)}) collective-permute-start(f32[2,16,30]{2,1,0:T(8,128)S(1)} %slice.378), channel_id=1, source_target_pairs={{1,0},{2,1},{3,2},{4,3},{5,4},{6,5},{7,6},{8,7},{9,8},{10,9},{11,1... | collective-permute-start | bytes 11528 | tf_op jit(solution)/shard_map/ppermute | solution.py:31
  53.4 1.8 %collective-permute-done = f32[2,16,30]{2,1,0:T(8,128)S(1)} collective-permute-done((f32[2,16,30]{2,1,0:T(8,128)S(1)}, f32[2,16,30]{2,1,0:T(8,128)S(1)}, u32[]{:S(2)}, u32[]{:S(2)}) %collective-permute-start) | collective-permute-done | bytes 3872 | tf_op jit(solution)/shard_map/ppermute | solution.py:31
  55.2 61.1 %while.45 = (s32[]{:T(128)}, f32[2,2,8192]{2,1,0:T(2,128)S(1)}, s32[]{:T(128)}, s32[4]{0:T(128)S(1)}, f32[2,16,8192]{2,1,0:T(8,128)S(1)}, /*index=5*/f32[2,16,30...) while((s32[]{:T(128)}, f32[2,2,8192]{2,1,0:T(2,128)S(1)}, ...), condition=%wide.region_21.22_spmd, body=%wide.region_12.21_spmd.sunk | while | flops 3301456 | bytes 33727040 | solution.py:155
  56.5 17.2 %conditional.4 = (f32[1,1,8192]{2,1,0:T(1,128)S(1)}) conditional(s32[]{:T(128)} %bitcast.327, () %tuple.181, (f32[16,8222]{1,0:T(8,128)S(1)}, s32[]{:T(128)}, s32[4,2,16]{2,1,0:T(2,128)}) %tuple.182), branch_computations={%region_14.14_spmd, %region_15.16_spmd} | conditional | flops 1576738 | bytes 15647118 | solution.py:145
  56.5 0.9 slice.271
  57.5 0.9 slice.270
  58.6 1.7 %slice.274 = f32[4,2,8222]{2,0,1:T(4,128)S(1)} slice(f32[8,2,8222]{2,0,1:T(8,128)S(1)} %pad_maximum_fusion), slice={[1:8:2], [0:2:1], [0:8222:1]} | slice | bytes 526208 | tf_op jit(solution)/shard_map/while/body/eval_jaxpr/cond/branch_1_fun/slice | solution.py:40
  60.3 1.7 %slice.272 = f32[4,2,8222]{2,0,1:T(4,128)S(1)} slice(f32[8,2,8222]{2,0,1:T(8,128)S(1)} %pad_maximum_fusion), slice={[0:8:2], [0:2:1], [0:8222:1]} | slice | bytes 526208 | tf_op jit(solution)/shard_map/while/body/eval_jaxpr/cond/branch_1_fun/slice | solution.py:39
  62.4 2.2 %slice.280 = f32[2,4,8222]{2,0,1:T(2,128)S(1)} slice(f32[4,4,8222]{2,0,1:T(4,128)S(1)} %pad_maximum_fusion.1), slice={[1:4:2], [0:4:1], [0:8222:1]} | slice | bytes 526208 | tf_op jit(solution)/shard_map/while/body/eval_jaxpr/cond/branch_1_fun/slice | solution.py:40
  64.6 2.2 %slice.278 = f32[2,4,8222]{2,0,1:T(2,128)S(1)} slice(f32[4,4,8222]{2,0,1:T(4,128)S(1)} %pad_maximum_fusion.1), slice={[0:4:2], [0:4:1], [0:8222:1]} | slice | bytes 526208 | tf_op jit(solution)/shard_map/while/body/eval_jaxpr/cond/branch_1_fun/slice | solution.py:39
  69.7 3.0 %stack.175 = f32[1,16,8222]{2,1,0:T(8,128)S(1)} concatenate(f32[1,1,8222]{2,1,0:T(1,128)S(1)} %get-tuple-element.436, f32[1,1,8222]{2,1,0:T(1,128)S(1)} %get-tuple-element.437, f32[1,1,8222]{2,1,0:T(1,128)S(1)} %get-tuple-element.427, f32[1,1,8222]{2,1,0:T(1,128)S(1)} %get-tuple-element.426, f32[1,1,8222]{2,1,0:T(1,128)S(1)} %get-tuple-element.434, ...), dimensions={1} | concatenate | bytes 1052416 | tf_op jit(solution)/shard_map/while/body/eval_jaxpr/cond/branch_1_fun/stack | solution.py:51
  78.4 17.2 %conditional.4 = (f32[1,1,8192]{2,1,0:T(1,128)S(1)}) conditional(s32[]{:T(128)} %bitcast.327, () %tuple.181, (f32[16,8222]{1,0:T(8,128)S(1)}, s32[]{:T(128)}, s32[4,2,16]{2,1,0:T(2,128)}) %tuple.182), branch_computations={%region_14.14_spmd, %region_15.16_spmd} | conditional | flops 1576738 | bytes 15647118 | solution.py:145
  78.5 0.9 slice.271
  79.4 0.9 slice.270
  80.6 1.7 %slice.274 = f32[4,2,8222]{2,0,1:T(4,128)S(1)} slice(f32[8,2,8222]{2,0,1:T(8,128)S(1)} %pad_maximum_fusion), slice={[1:8:2], [0:2:1], [0:8222:1]} | slice | bytes 526208 | tf_op jit(solution)/shard_map/while/body/eval_jaxpr/cond/branch_1_fun/slice | solution.py:40
  82.3 1.7 %slice.272 = f32[4,2,8222]{2,0,1:T(4,128)S(1)} slice(f32[8,2,8222]{2,0,1:T(8,128)S(1)} %pad_maximum_fusion), slice={[0:8:2], [0:2:1], [0:8222:1]} | slice | bytes 526208 | tf_op jit(solution)/shard_map/while/body/eval_jaxpr/cond/branch_1_fun/slice | solution.py:39
  84.4 2.2 %slice.280 = f32[2,4,8222]{2,0,1:T(2,128)S(1)} slice(f32[4,4,8222]{2,0,1:T(4,128)S(1)} %pad_maximum_fusion.1), slice={[1:4:2], [0:4:1], [0:8222:1]} | slice | bytes 526208 | tf_op jit(solution)/shard_map/while/body/eval_jaxpr/cond/branch_1_fun/slice | solution.py:40
  86.6 2.2 %slice.278 = f32[2,4,8222]{2,0,1:T(2,128)S(1)} slice(f32[4,4,8222]{2,0,1:T(4,128)S(1)} %pad_maximum_fusion.1), slice={[0:4:2], [0:4:1], [0:8222:1]} | slice | bytes 526208 | tf_op jit(solution)/shard_map/while/body/eval_jaxpr/cond/branch_1_fun/slice | solution.py:39
  91.7 3.0 %stack.175 = f32[1,16,8222]{2,1,0:T(8,128)S(1)} concatenate(f32[1,1,8222]{2,1,0:T(1,128)S(1)} %get-tuple-element.436, f32[1,1,8222]{2,1,0:T(1,128)S(1)} %get-tuple-element.437, f32[1,1,8222]{2,1,0:T(1,128)S(1)} %get-tuple-element.427, f32[1,1,8222]{2,1,0:T(1,128)S(1)} %get-tuple-element.426, f32[1,1,8222]{2,1,0:T(1,128)S(1)} %get-tuple-element.434, ...), dimensions={1} | concatenate | bytes 1052416 | tf_op jit(solution)/shard_map/while/body/eval_jaxpr/cond/branch_1_fun/stack | solution.py:51
  98.0 17.2 %conditional.5 = (f32[1,1,8192]{2,1,0:T(1,128)S(1)}) conditional(s32[]{:T(128)} %bitcast.329, () %tuple.183, (f32[16,8222]{1,0:T(8,128)S(1)}, s32[]{:T(128)}, s32[4,2,16]{2,1,0:T(2,128)}) %tuple.182), branch_computations={%region_18.18_spmd, %region_19.20_spmd} | conditional | flops 1576738 | bytes 15647118 | solution.py:145
  98.1 0.9 slice.307
  100.2 1.7 %slice.310 = f32[4,2,8222]{2,0,1:T(4,128)S(1)} slice(f32[8,2,8222]{2,0,1:T(8,128)S(1)} %pad_maximum_fusion.2), slice={[1:8:2], [0:2:1], [0:8222:1]} | slice | bytes 526208 | tf_op jit(solution)/shard_map/while/body/eval_jaxpr/cond/branch_1_fun/slice | solution.py:40
  101.9 1.7 %slice.308 = f32[4,2,8222]{2,0,1:T(4,128)S(1)} slice(f32[8,2,8222]{2,0,1:T(8,128)S(1)} %pad_maximum_fusion.2), slice={[0:8:2], [0:2:1], [0:8222:1]} | slice | bytes 526208 | tf_op jit(solution)/shard_map/while/body/eval_jaxpr/cond/branch_1_fun/slice | solution.py:39
  104.0 2.2 %slice.316 = f32[2,4,8222]{2,0,1:T(2,128)S(1)} slice(f32[4,4,8222]{2,0,1:T(4,128)S(1)} %pad_maximum_fusion.3), slice={[1:4:2], [0:4:1], [0:8222:1]} | slice | bytes 526208 | tf_op jit(solution)/shard_map/while/body/eval_jaxpr/cond/branch_1_fun/slice | solution.py:40
  106.2 2.2 %slice.314 = f32[2,4,8222]{2,0,1:T(2,128)S(1)} slice(f32[4,4,8222]{2,0,1:T(4,128)S(1)} %pad_maximum_fusion.3), slice={[0:4:2], [0:4:1], [0:8222:1]} | slice | bytes 526208 | tf_op jit(solution)/shard_map/while/body/eval_jaxpr/cond/branch_1_fun/slice | solution.py:39
  111.3 3.0 %stack.209 = f32[1,16,8222]{2,1,0:T(8,128)S(1)} concatenate(f32[1,1,8222]{2,1,0:T(1,128)S(1)} %get-tuple-element.482, f32[1,1,8222]{2,1,0:T(1,128)S(1)} %get-tuple-element.483, f32[1,1,8222]{2,1,0:T(1,128)S(1)} %get-tuple-element.473, f32[1,1,8222]{2,1,0:T(1,128)S(1)} %get-tuple-element.472, f32[1,1,8222]{2,1,0:T(1,128)S(1)} %get-tuple-element.480, ...), dimensions={1} | concatenate | bytes 1052416 | tf_op jit(solution)/shard_map/while/body/eval_jaxpr/cond/branch_1_fun/stack | solution.py:51
  116.6 6.8 %all_to_all.5 = f32[2,2,1,8192]{3,2,1,0:T(1,128)S(1)} all-to-all(f32[2,2,1,8192]{3,2,1,0:T(1,128)S(1)} %pad_maximum_fusion.5), channel_id=1, replica_groups=mesh['section'=2,'freq'=16] {'section'}, dimensions={0} | all-to-all | bytes 262144 | tf_op jit(solution)/shard_map/all_to_all | solution.py:10
  (174 shorter events, 31.8 us)
Async XLA Ops:
  0.0 0.8 copy-start.1
  0.8 51.1 %copy-start = (f32[2,16,8192]{2,1,0:T(8,128)S(1)}, f32[2,16,8192]{2,1,0:T(8,128)}, u32[]{:S(2)}) copy-start(f32[2,16,8192]{2,1,0:T(8,128)} %param.19) | copy-start | bytes 3145732
  40.8 0.7 copy-start.4
  52.1 3.1 %collective-permute-start = (f32[2,16,30]{2,1,0:T(8,128)S(1)}, f32[2,16,30]{2,1,0:T(8,128)S(1)}, u32[]{:S(2)}, u32[]{:S(2)}) collective-permute-start(f32[2,16,30]{2,1,0:T(8,128)S(1)} %slice.378), channel_id=1, source_target_pairs={{1,0},{2,1},{3,2},{4,3},{5,4},{6,5},{7,6},{8,7},{9,8},{10,9},{11,1... | collective-permute-start | bytes 11528 | tf_op jit(solution)/shard_map/ppermute | solution.py:31
  53.4 1.8 %copy-start.2 = (s32[3]{0:T(128)S(1)}, s32[3]{0:T(128)}, u32[]{:S(2)}) copy-start(s32[3]{0:T(128)} %constant.199.clone.1) | copy-start | bytes 40
  53.4 1.8 %copy-start.3 = (s32[4]{0:T(128)S(1)}, s32[4]{0:T(128)}, u32[]{:S(2)}) copy-start(s32[4]{0:T(128)} %param.22) | copy-start | bytes 52
